TPU v7x, 32 devices: a whole 2x2x4 slice. The times are simulated.
32 devices in a mesh: dom: 8 (over z, y), level: 4 (over x, core).
Axes of the slice: x: 2, y: 2, z: 4, core: 2. Of those that a mesh axis runs over, the one named last changes fastest.
Arguments:
- dg_values: bfloat16 [98304, 384], P(('dom', 'level')), may hold values from -6 to 6
- stiff_mu: bfloat16 [384, 384], replicated, may hold values from -0.1 to 2, as said below
- stiff_lam: bfloat16 [384, 384], replicated, may hold values from -0.1 to 2, as said below
- coef_mu: float32 [98304], P(('dom', 'level')), may hold values from 0.25 to 4
- coef_lam: float32 [98304], P(('dom', 'level')), may hold values from 0.25 to 4
- elem_count: int32 [32], P(('dom', 'level')), may hold values from 384 to 3072, as said below
- elem_block: int32 [3, 98304], P(None, ('dom', 'level')), may hold values from 0 to 1023
- share_map: int32 [32, 8, 32], P(('dom', 'level')), may hold values from 0 to 1024, as said below
- hang_child: int32 [32, 64], P(('dom', 'level')), may hold values from 0 to 1024, as said below
- hang_parent: int32 [32, 64, 2], P(('dom', 'level')), may hold values from 0 to 1023
Outputs:
- projected: float32 [3, 32768, 128], P(None, ('dom', 'level'))
- energy: float32 [], replicated
Inputs may be any that keep to these rules, and one draw needn't show every extreme that they name: `elem_count`: between 384 and 3072; one device, drawn anew, holds exactly 3072. `share_map`: Slots agree in pairs: [d, o, s] is live exactly when the partner's [d2, o', s] is live, and they name the same DoF block. Slots toward ranks outside 0 to 7 are empty. For every offset some rank pair fills all 32 slots. `hang_child`: on each device of level index 1 or more, 64 distinct blocks below 1024; on devices of level index 0 every entry is 1024 (no hanging blocks). `hang_parent`: block numbers on the device of the same rank and the next lower level index; unused on level index 0. `stiff_mu`: Symmetric. `stiff_lam`: Symmetric.
All inputs are finite; a program needn't handle non-finite values.
Results may differ from a plain program's by a relative error of at most 0.0003.
Values sent between devices are 32-bit elements; how exact they have to be, the bound alone decides.
A program may use at most 64 MiB of HBM per device.

v0:
```python
import jax
import jax.numpy as jnp
from jax import lax
from jax.sharding import PartitionSpec as P


def from_behind(block, axis, distance):
    devices = range(lax.axis_size(axis))
    route = [(i - distance, i) for i in devices if i - distance in devices]
    return lax.ppermute(block, axis, route)


def shards(
    dg_values,
    stiff_mu,
    stiff_lam,
    coef_mu,
    coef_lam,
    elem_count,
    elem_block,
    share_map,
    hang_child,
    hang_parent,
):
    elements = dg_values.shape[0]
    row_width = stiff_mu.shape[0]
    block_size = row_width // 3
    block_count = elements // 3
    offsets_half = share_map.shape[1] // 2
    joined = jnp.concatenate((stiff_mu, stiff_lam), axis=1)
    product = jnp.dot(dg_values, joined, preferred_element_type=jnp.float32)
    forces = coef_mu[:, None] * product[:, :row_width] + coef_lam[:, None] * product[:, row_width:]
    live_rows = jnp.arange(elements) < elem_count[0]
    forces = jnp.where(live_rows[:, None], forces, jnp.float32(0.0))
    energy_part = 0.5 * jnp.sum(dg_values.astype(jnp.float32) * forces)
    component_forces = jnp.transpose(forces.reshape(elements, 3, block_size), (1, 0, 2))
    block_ids = jnp.arange(block_count + 1, dtype=jnp.int32)

    def sum_blocks(packed):
        target_ids, component_part = packed
        selector = (block_ids[:, None] == target_ids[None, :]).astype(jnp.float32)
        return jnp.dot(
            selector,
            component_part,
            precision=lax.Precision.HIGHEST,
            preferred_element_type=jnp.float32,
        )

    local_blocks = lax.map(sum_blocks, (elem_block, component_forces))
    slot_blocks = share_map[0]
    outgoing = jnp.transpose(local_blocks[:, slot_blocks, :], (1, 0, 2, 3))
    offsets = [step + 1 for step in range(offsets_half)] + [
        -(step + 1) for step in range(offsets_half)
    ]
    pieces = [None] * (2 * offsets_half)
    for slot_index in range(2 * offsets_half):
        opposite = (slot_index + offsets_half) % (2 * offsets_half)
        pieces[opposite] = from_behind(outgoing[slot_index], "dom", offsets[slot_index])
    incoming = jnp.stack(pieces)
    received = jnp.transpose(incoming, (1, 0, 2, 3)).reshape(3, -1, block_size)
    assembled = local_blocks.at[:, slot_blocks.reshape(-1), :].add(received)
    wanted = from_behind(hang_parent, "level", -1)
    chosen = assembled[:, wanted[0].reshape(-1), :]
    picked = from_behind(chosen, "level", 1)
    parent_pairs = picked.reshape(3, -1, 2, block_size)
    child_values = 0.5 * (parent_pairs[:, :, 0] + parent_pairs[:, :, 1])
    projected = assembled.at[:, hang_child[0], :].set(child_values)
    scale_total = jnp.float32(row_width * elements * lax.axis_size("dom") * lax.axis_size("level"))
    energy = lax.psum(energy_part, ("dom", "level")) / scale_total
    return (projected[:, :block_count], energy)


def solution(mesh):
    return jax.shard_map(
        shards,
        mesh=mesh,
        in_specs=(
            P(("dom", "level"), None),
            P(),
            P(),
            P(("dom", "level")),
            P(("dom", "level")),
            P(("dom", "level")),
            P(None, ("dom", "level")),
            P(("dom", "level"), None, None),
            P(("dom", "level"), None),
            P(("dom", "level"), None, None),
        ),
        out_specs=(P(None, ("dom", "level"), None), P()),
        check_vma=False,
    )
```

profile of v0, /device:TPU:18, one launch (start us, length us, event | category | flops | bytes accessed | tf_op | source)
XLA Modules:
  0.0 186.4 jit_solution(15404276880878706162)
XLA Ops:
  0.6 1.9 %collective-permute-start.8 = (s32[1,64,2]{1,2,0:T(2,128)}, s32[1,64,2]{1,2,0:T(2,128)S(1)}, u32[]{:S(2)}, u32[]{:S(2)}) collective-permute-start(s32[1,64,2]{1,2,0:T(2,128)} %param.21), channel_id=1, source_target_pairs={{1,0},{2,1},{3,2},{5,4},{6,5},{7,6},{9,8},{10,9},{11,10},{13,12},{... | collective-permute-start | bytes 1544 | tf_op jit(solution)/shard_map/ppermute | solution.py:10
  2.6 0.0 copy-start
  2.6 0.0 copy-start.3
  2.6 0.0 copy-start.4
  2.6 4.4 %copy.33 = bf16[3072,384]{0,1:T(8,128)(2,1)} copy(bf16[3072,384]{1,0:T(8,128)(2,1)} %param.12) | data formatting | bytes 4718592 | tf_op args[0]
  7.7 0.0 copy-done
  7.7 0.0 copy-done.3
  7.7 0.0 copy-done.4
  7.7 0.0 copy-start.1
  7.7 0.0 copy-start.6
  7.7 0.0 copy-start.7
  7.8 2.7 %convolution_bitcast_fusion = f32[3072,768]{0,1:T(8,128)S(1)} fusion(bf16[3072,384]{1,0:T(8,128)(2,1)S(1)} %copy-done, bf16[384,384]{1,0:T(8,128)(2,1)S(1)} %copy-done.3, bf16[384,384]{1,0:T(8,128)(2,1)S(1)} %copy-done.4), kind=kOutput, calls=%fused_computation.13 | convolution fusion | flops 1813118976 | bytes 12386304 | tf_op jit(solution)/shard_map/dot_general | solution.py:31
  10.4 0.0 copy-done.1
  10.4 0.0 copy-done.6
  10.4 0.0 copy-done.7
  10.4 4.5 %multiply_reduce_fusion = (f32[]{:T(128)}, f32[3072,384]{0,1:T(8,128)}) fusion(bf16[3072,384]{0,1:T(8,128)(2,1)S(1)} %copy-done.1, f32[3072,768]{0,1:T(8,128)S(1)} %convolution_bitcast_fusion, f32[3072]{0:T(1024)S(1)} %copy-done.6, f32[3072]{0:T(1024)S(1)} %copy-done.7, pred[3072]{0:T(1024)(128)(4,1)S(1)} %iota_compare_fusion.4), kind=kLoop, calls=%fused_computation.18 | loop fusion | flops 8257535 | bytes 16542724 | tf_op jit(solution)/shard_map/reduce_sum | solution.py:35
  14.9 6.2 %copy.27 = f32[3072,3,128]{2,0,1:T(8,128)} copy(f32[3072,3,128]{0,2,1:T(8,128)} %bitcast.88) | data formatting | bytes 9437184 | tf_op jit(solution)/shard_map/reshape | solution.py:36
  21.1 0.0 copy-done.2
  21.1 73.7 %while.11 = (s32[]{:T(128)}, f32[3,1025,128]{2,0,1:T(4,128)S(1)}, s32[3,3072]{1,0:T(4,128)}, f32[3,3072,128]{2,1,0:T(8,128)}, s32[]{:T(128)}, /*index=5*/s32[]{:T(128)}) while((s32[]{:T(128)}, f32[3,1025,128]{2,0,1:T(4,128)S(1)}, s32[3,3072]{1,0:T(4,128)}, f32[3,3072,128]{2,1,0:T(8,128)}, s32[]{:T(128)}, /*index=5*/s32[]{:T(128)}) %tuple.40), condition=%wide.region_1.2_spmd.clone, body=%wide.region_0.1_spmd.clone.sunk | while | flops 4839705600 | bytes 4234317 | solution.py:49
  21.1 0.8 constant_dynamic-slice_fusion.2
  21.9 7.2 %fusion.24 = f32[1,1025,128]{2,1,0:T(8,128)S(1)} fusion(s32[3072]{0:T(1024)S(1)} %bitcast.92, f32[3,3072,128]{2,1,0:T(8,128)} %get-tuple-element.104, s32[]{:T(128)} %get-tuple-element.95), kind=kOutput, calls=%fused_computation.8.clone.1 | convolution fusion | flops 4839705600 | bytes 2110464 | tf_op jit(solution)/shard_map/while/body/eval_jaxpr/dot_general | solution.py:42
  29.1 3.3 %copy.41 = f32[1,1025,128]{2,0,1:T(1,128)S(1)} copy(f32[1,1025,128]{2,1,0:T(8,128)S(1)} %fusion.24) | data formatting | bytes 1049600 | tf_op jit(solution)/shard_map/while/body/jit(dynamic_update_index_in_dim)/dynamic_update_slice | solution.py:49
  32.4 13.2 %dynamic_update_slice.6 = f32[3,1025,128]{2,0,1:T(4,128)S(1)} dynamic-update-slice(f32[3,1025,128]{2,0,1:T(4,128)S(1)} %get-tuple-element.96, f32[1,1025,128]{2,0,1:T(1,128)S(1)} %copy.41, s32[]{:T(128)} %get-tuple-element.95, s32[]{:T(128)} %constant.11.clone.1..sunk, s32[]{:T(128)} %constant.11.clone.1..sunk) | dynamic-update-slice | bytes 1049604 | tf_op jit(solution)/shard_map/while/body/jit(dynamic_update_index_in_dim)/dynamic_update_slice | solution.py:49
  45.7 0.8 constant_dynamic-slice_fusion.2
  46.5 7.2 %fusion.24 = f32[1,1025,128]{2,1,0:T(8,128)S(1)} fusion(s32[3072]{0:T(1024)S(1)} %bitcast.92, f32[3,3072,128]{2,1,0:T(8,128)} %get-tuple-element.104, s32[]{:T(128)} %get-tuple-element.95), kind=kOutput, calls=%fused_computation.8.clone.1 | convolution fusion | flops 4839705600 | bytes 2110464 | tf_op jit(solution)/shard_map/while/body/eval_jaxpr/dot_general | solution.py:42
  53.7 3.3 %copy.41 = f32[1,1025,128]{2,0,1:T(1,128)S(1)} copy(f32[1,1025,128]{2,1,0:T(8,128)S(1)} %fusion.24) | data formatting | bytes 1049600 | tf_op jit(solution)/shard_map/while/body/jit(dynamic_update_index_in_dim)/dynamic_update_slice | solution.py:49
  57.0 13.2 %dynamic_update_slice.6 = f32[3,1025,128]{2,0,1:T(4,128)S(1)} dynamic-update-slice(f32[3,1025,128]{2,0,1:T(4,128)S(1)} %get-tuple-element.96, f32[1,1025,128]{2,0,1:T(1,128)S(1)} %copy.41, s32[]{:T(128)} %get-tuple-element.95, s32[]{:T(128)} %constant.11.clone.1..sunk, s32[]{:T(128)} %constant.11.clone.1..sunk) | dynamic-update-slice | bytes 1049604 | tf_op jit(solution)/shard_map/while/body/jit(dynamic_update_index_in_dim)/dynamic_update_slice | solution.py:49
  70.2 0.8 constant_dynamic-slice_fusion.2
  71.0 7.2 %fusion.24 = f32[1,1025,128]{2,1,0:T(8,128)S(1)} fusion(s32[3072]{0:T(1024)S(1)} %bitcast.92, f32[3,3072,128]{2,1,0:T(8,128)} %get-tuple-element.104, s32[]{:T(128)} %get-tuple-element.95), kind=kOutput, calls=%fused_computation.8.clone.1 | convolution fusion | flops 4839705600 | bytes 2110464 | tf_op jit(solution)/shard_map/while/body/eval_jaxpr/dot_general | solution.py:42
  78.2 3.3 %copy.41 = f32[1,1025,128]{2,0,1:T(1,128)S(1)} copy(f32[1,1025,128]{2,1,0:T(8,128)S(1)} %fusion.24) | data formatting | bytes 1049600 | tf_op jit(solution)/shard_map/while/body/jit(dynamic_update_index_in_dim)/dynamic_update_slice | solution.py:49
  81.5 13.2 %dynamic_update_slice.6 = f32[3,1025,128]{2,0,1:T(4,128)S(1)} dynamic-update-slice(f32[3,1025,128]{2,0,1:T(4,128)S(1)} %get-tuple-element.96, f32[1,1025,128]{2,0,1:T(1,128)S(1)} %copy.41, s32[]{:T(128)} %get-tuple-element.95, s32[]{:T(128)} %constant.11.clone.1..sunk, s32[]{:T(128)} %constant.11.clone.1..sunk) | dynamic-update-slice | bytes 1049604 | tf_op jit(solution)/shard_map/while/body/jit(dynamic_update_index_in_dim)/dynamic_update_slice | solution.py:49
  94.8 0.0 copy-done.5
  94.8 0.0 copy-start.8
  94.8 0.1 reshape_squeeze.6
  94.9 0.1 reshape.140
  95.6 0.0 collective-permute-done.8
  95.6 0.1 copy.30
  95.7 0.1 reshape_squeeze.7
  95.9 1.0 gather_fusion
  96.9 0.1 slice_bitcast_fusion.2
  97.0 3.3 %collective-permute-start = (f32[3,32,128]{2,0,1:T(4,128)S(1)}, f32[3,32,128]{2,0,1:T(4,128)S(1)}, u32[]{:S(2)}, u32[]{:S(2)}) collective-permute-start(f32[3,32,128]{2,0,1:T(4,128)S(1)} %get-tuple-element.61), channel_id=1, source_target_pairs={{4,0},{8,4},{12,8},{16,12},{20,16},{24,20},{28,24},{5,1},{9,5},{13... | collective-permute-start | bytes 147464 | tf_op jit(solution)/shard_map/ppermute | solution.py:10
  100.3 40.1 %psum.7 = f32[]{:T(128)} all-reduce(f32[]{:T(128)S(6)} %mul.39), channel_id=1, replica_groups=mesh['dom'=8,'level'=4] {'dom','level'}, use_global_device_ids=true, to_apply=%region_5.6 | all-reduce | flops 1 | bytes 8 | tf_op jit(solution)/shard_map/psum | solution.py:69
  141.1 2.5 %collective-permute-start.1 = (f32[3,32,128]{2,0,1:T(4,128)S(1)}, f32[3,32,128]{2,0,1:T(4,128)S(1)}, u32[]{:S(2)}, u32[]{:S(2)}) collective-permute-start(f32[3,32,128]{2,0,1:T(4,128)S(1)} %get-tuple-element.60), channel_id=1, source_target_pairs={{8,0},{12,4},{16,8},{20,12},{24,16},{28,20},{9,1},{13,5},{17,9},{2... | collective-permute-start | bytes 147464 | tf_op jit(solution)/shard_map/ppermute | solution.py:10
  143.7 2.2 %collective-permute-start.2 = (f32[3,32,128]{2,0,1:T(4,128)S(1)}, f32[3,32,128]{2,0,1:T(4,128)S(1)}, u32[]{:S(2)}, u32[]{:S(2)}) collective-permute-start(f32[3,32,128]{2,0,1:T(4,128)S(1)} %get-tuple-element.59), channel_id=1, source_target_pairs={{12,0},{16,4},{20,8},{24,12},{28,16},{13,1},{17,5},{21,9},{25,13},... | collective-permute-start | bytes 147464 | tf_op jit(solution)/shard_map/ppermute | solution.py:10
  145.9 1.3 collective-permute-start.3
  147.2 3.6 %collective-permute-start.4 = (f32[3,32,128]{2,0,1:T(4,128)S(1)}, f32[3,32,128]{2,0,1:T(4,128)S(1)}, u32[]{:S(2)}, u32[]{:S(2)}) collective-permute-start(f32[3,32,128]{2,0,1:T(4,128)S(1)} %get-tuple-element.57), channel_id=1, source_target_pairs={{0,4},{4,8},{8,12},{12,16},{16,20},{20,24},{24,28},{1,5},{5,9},{9,... | collective-permute-start | bytes 147464 | tf_op jit(solution)/shard_map/ppermute | solution.py:10
  150.8 0.0 collective-permute-done
  150.8 4.1 %collective-permute-start.5 = (f32[3,32,128]{2,0,1:T(4,128)S(1)}, f32[3,32,128]{2,0,1:T(4,128)S(1)}, u32[]{:S(2)}, u32[]{:S(2)}) collective-permute-start(f32[3,32,128]{2,0,1:T(4,128)S(1)} %get-tuple-element.56), channel_id=1, source_target_pairs={{0,8},{4,12},{8,16},{12,20},{16,24},{20,28},{1,9},{5,13},{9,17},{1... | collective-permute-start | bytes 147464 | tf_op jit(solution)/shard_map/ppermute | solution.py:10
  154.9 0.0 collective-permute-done.1
  154.9 1.9 %collective-permute-start.6 = (f32[3,32,128]{2,0,1:T(4,128)S(1)}, f32[3,32,128]{2,0,1:T(4,128)S(1)}, u32[]{:S(2)}, u32[]{:S(2)}) collective-permute-start(f32[3,32,128]{2,0,1:T(4,128)S(1)} %get-tuple-element.55), channel_id=1, source_target_pairs={{0,12},{4,16},{8,20},{12,24},{16,28},{1,13},{5,17},{9,21},{13,25},... | collective-permute-start | bytes 147464 | tf_op jit(solution)/shard_map/ppermute | solution.py:10
  156.9 0.0 collective-permute-done.2
  156.9 1.3 collective-permute-start.7
  158.2 0.0 collective-permute-done.3
  158.2 0.0 collective-permute-done.4
  158.3 0.0 collective-permute-done.5
  158.3 4.7 %collective-permute-done.6 = f32[3,32,128]{2,0,1:T(4,128)S(1)} collective-permute-done((f32[3,32,128]{2,0,1:T(4,128)S(1)}, f32[3,32,128]{2,0,1:T(4,128)S(1)}, u32[]{:S(2)}, u32[]{:S(2)}) %collective-permute-start.6) | collective-permute-done | bytes 49184 | tf_op jit(solution)/shard_map/ppermute | solution.py:10
  163.0 0.9 collective-permute-done.7
  163.9 8.8 %scatter_fusion = f32[3,1025,128]{2,0,1:T(4,128)S(1)} fusion(f32[3,1025,128]{2,0,1:T(4,128)S(1)} %get-tuple-element.29, s32[256]{0:T(256)S(1)} %bitcast.95, f32[256,3,128]{2,1,0:T(4,128)S(1)} %bitcast.91), kind=kCustom, calls=%fused_computation.2 | custom fusion | flops 98304 | bytes 1180672 | tf_op jit(solution)/shard_map/scatter-add | solution.py:61
  172.7 0.8 gather_fusion.1
  173.5 1.9 %collective-permute-start.9 = (f32[3,128,128]{2,0,1:T(4,128)S(1)}, f32[3,128,128]{2,0,1:T(4,128)S(1)}, u32[]{:S(2)}, u32[]{:S(2)}) collective-permute-start(f32[3,128,128]{2,0,1:T(4,128)S(1)} %bitcast.94), channel_id=1, source_target_pairs={{0,1},{1,2},{2,3},{4,5},{5,6},{6,7},{8,9},{9,10},{10,11},{12,13},{... | collective-permute-start | bytes 589832 | tf_op jit(solution)/shard_map/ppermute | solution.py:10
  175.5 5.7 %collective-permute-done.9 = f32[3,128,128]{2,0,1:T(4,128)S(1)} collective-permute-done((f32[3,128,128]{2,0,1:T(4,128)S(1)}, f32[3,128,128]{2,0,1:T(4,128)S(1)}, u32[]{:S(2)}, u32[]{:S(2)}) %collective-permute-start.9) | collective-permute-done | bytes 196640 | tf_op jit(solution)/shard_map/ppermute | solution.py:10
  181.2 2.4 %scatter_fusion.1 = f32[3,1025,128]{2,0,1:T(4,128)S(1)} fusion(f32[3,1025,128]{2,0,1:T(4,128)S(1)} %scatter_fusion, s32[64]{0:T(128)S(1)} %fusion.16, f32[64,3,128]{2,1,0:T(4,128)S(1)} %fusion.15), kind=kCustom, calls=%fused_computation.3 | custom fusion | bytes 295168 | tf_op jit(solution)/shard_map/scatter | solution.py:67
  183.7 0.4 slice.68
  184.1 1.2 copy.34
  (19 shorter events, 0.2 us)
Async XLA Ops:
  0.6 95.0 %collective-permute-start.8 = (s32[1,64,2]{1,2,0:T(2,128)}, s32[1,64,2]{1,2,0:T(2,128)S(1)}, u32[]{:S(2)}, u32[]{:S(2)}) collective-permute-start(s32[1,64,2]{1,2,0:T(2,128)} %param.21), channel_id=1, source_target_pairs={{1,0},{2,1},{3,2},{5,4},{6,5},{7,6},{9,8},{10,9},{11,10},{13,12},{... | collective-permute-start | bytes 1544 | tf_op jit(solution)/shard_map/ppermute | solution.py:10
  2.6 5.1 %copy-start = (bf16[3072,384]{1,0:T(8,128)(2,1)S(1)}, bf16[3072,384]{1,0:T(8,128)(2,1)}, u32[]{:S(2)}) copy-start(bf16[3072,384]{1,0:T(8,128)(2,1)} %param.12) | copy-start | bytes 7077892
  2.6 5.1 %copy-start.3 = (bf16[384,384]{1,0:T(8,128)(2,1)S(1)}, bf16[384,384]{1,0:T(8,128)(2,1)}, u32[]{:S(2)}) copy-start(bf16[384,384]{1,0:T(8,128)(2,1)} %param.14) | copy-start | bytes 884740
  2.6 5.1 %copy-start.4 = (bf16[384,384]{1,0:T(8,128)(2,1)S(1)}, bf16[384,384]{1,0:T(8,128)(2,1)}, u32[]{:S(2)}) copy-start(bf16[384,384]{1,0:T(8,128)(2,1)} %param.13) | copy-start | bytes 884740
  7.7 2.7 %copy-start.1 = (bf16[3072,384]{0,1:T(8,128)(2,1)S(1)}, bf16[3072,384]{0,1:T(8,128)(2,1)}, u32[]{:S(2)}) copy-start(bf16[3072,384]{0,1:T(8,128)(2,1)} %copy.33) | copy-start | bytes 7077892
  7.7 2.7 %copy-start.6 = (f32[3072]{0:T(1024)S(1)}, f32[3072]{0:T(1024)}, u32[]{:S(2)}) copy-start(f32[3072]{0:T(1024)} %param.16) | copy-start | bytes 36868
  7.7 2.7 %copy-start.7 = (f32[3072]{0:T(1024)S(1)}, f32[3072]{0:T(1024)}, u32[]{:S(2)}) copy-start(f32[3072]{0:T(1024)} %param.15) | copy-start | bytes 36868
  14.9 6.2 %copy-start.2 = (f32[3,1025,128]{2,0,1:T(4,128)S(1)}, f32[3,1025,128]{2,0,1:T(4,128)}, u32[]{:S(2)}) copy-start(f32[3,1025,128]{2,0,1:T(4,128)} %custom-call.5) | copy-start | bytes 4723204
  21.1 73.7 %copy-start.5 = (s32[1,8,32]{2,1,0:T(8,128)S(1)}, s32[1,8,32]{2,1,0:T(8,128)}, u32[]{:S(2)}) copy-start(s32[1,8,32]{2,1,0:T(8,128)} %param.19) | copy-start | bytes 3076
  94.8 80.6 %copy-start.8 = (s32[1,64]{1,0:T(1,128)S(1)}, s32[1,64]{1,0:T(1,128)}, u32[]{:S(2)}) copy-start(s32[1,64]{1,0:T(1,128)} %param.20) | copy-start | bytes 772
  97.0 53.8 %collective-permute-start = (f32[3,32,128]{2,0,1:T(4,128)S(1)}, f32[3,32,128]{2,0,1:T(4,128)S(1)}, u32[]{:S(2)}, u32[]{:S(2)}) collective-permute-start(f32[3,32,128]{2,0,1:T(4,128)S(1)} %get-tuple-element.61), channel_id=1, source_target_pairs={{4,0},{8,4},{12,8},{16,12},{20,16},{24,20},{28,24},{5,1},{9,5},{13... | collective-permute-start | bytes 147464 | tf_op jit(solution)/shard_map/ppermute | solution.py:10
  141.1 13.8 %collective-permute-start.1 = (f32[3,32,128]{2,0,1:T(4,128)S(1)}, f32[3,32,128]{2,0,1:T(4,128)S(1)}, u32[]{:S(2)}, u32[]{:S(2)}) collective-permute-start(f32[3,32,128]{2,0,1:T(4,128)S(1)} %get-tuple-element.60), channel_id=1, source_target_pairs={{8,0},{12,4},{16,8},{20,12},{24,16},{28,20},{9,1},{13,5},{17,9},{2... | collective-permute-start | bytes 147464 | tf_op jit(solution)/shard_map/ppermute | solution.py:10
  143.7 13.2 %collective-permute-start.2 = (f32[3,32,128]{2,0,1:T(4,128)S(1)}, f32[3,32,128]{2,0,1:T(4,128)S(1)}, u32[]{:S(2)}, u32[]{:S(2)}) collective-permute-start(f32[3,32,128]{2,0,1:T(4,128)S(1)} %get-tuple-element.59), channel_id=1, source_target_pairs={{12,0},{16,4},{20,8},{24,12},{28,16},{13,1},{17,5},{21,9},{25,13},... | collective-permute-start | bytes 147464 | tf_op jit(solution)/shard_map/ppermute | solution.py:10
  145.9 12.3 %collective-permute-start.3 = (f32[3,32,128]{2,0,1:T(4,128)S(1)}, f32[3,32,128]{2,0,1:T(4,128)S(1)}, u32[]{:S(2)}, u32[]{:S(2)}) collective-permute-start(f32[3,32,128]{2,0,1:T(4,128)S(1)} %get-tuple-element.58), channel_id=1, source_target_pairs={{16,0},{20,4},{24,8},{28,12},{17,1},{21,5},{25,9},{29,13},{18,2},{... | collective-permute-start | bytes 147464 | tf_op jit(solution)/shard_map/ppermute | solution.py:10
  147.2 11.0 %collective-permute-start.4 = (f32[3,32,128]{2,0,1:T(4,128)S(1)}, f32[3,32,128]{2,0,1:T(4,128)S(1)}, u32[]{:S(2)}, u32[]{:S(2)}) collective-permute-start(f32[3,32,128]{2,0,1:T(4,128)S(1)} %get-tuple-element.57), channel_id=1, source_target_pairs={{0,4},{4,8},{8,12},{12,16},{16,20},{20,24},{24,28},{1,5},{5,9},{9,... | collective-permute-start | bytes 147464 | tf_op jit(solution)/shard_map/ppermute | solution.py:10
  150.8 7.5 %collective-permute-start.5 = (f32[3,32,128]{2,0,1:T(4,128)S(1)}, f32[3,32,128]{2,0,1:T(4,128)S(1)}, u32[]{:S(2)}, u32[]{:S(2)}) collective-permute-start(f32[3,32,128]{2,0,1:T(4,128)S(1)} %get-tuple-element.56), channel_id=1, source_target_pairs={{0,8},{4,12},{8,16},{12,20},{16,24},{20,28},{1,9},{5,13},{9,17},{1... | collective-permute-start | bytes 147464 | tf_op jit(solution)/shard_map/ppermute | solution.py:10
  154.9 8.1 %collective-permute-start.6 = (f32[3,32,128]{2,0,1:T(4,128)S(1)}, f32[3,32,128]{2,0,1:T(4,128)S(1)}, u32[]{:S(2)}, u32[]{:S(2)}) collective-permute-start(f32[3,32,128]{2,0,1:T(4,128)S(1)} %get-tuple-element.55), channel_id=1, source_target_pairs={{0,12},{4,16},{8,20},{12,24},{16,28},{1,13},{5,17},{9,21},{13,25},... | collective-permute-start | bytes 147464 | tf_op jit(solution)/shard_map/ppermute | solution.py:10
  156.9 7.1 %collective-permute-start.7 = (f32[3,32,128]{2,0,1:T(4,128)S(1)}, f32[3,32,128]{2,0,1:T(4,128)S(1)}, u32[]{:S(2)}, u32[]{:S(2)}) collective-permute-start(f32[3,32,128]{2,0,1:T(4,128)S(1)} %get-tuple-element.54), channel_id=1, source_target_pairs={{0,16},{4,20},{8,24},{12,28},{1,17},{5,21},{9,25},{13,29},{2,18},{... | collective-permute-start | bytes 147464 | tf_op jit(solution)/shard_map/ppermute | solution.py:10
  173.5 7.7 %collective-permute-start.9 = (f32[3,128,128]{2,0,1:T(4,128)S(1)}, f32[3,128,128]{2,0,1:T(4,128)S(1)}, u32[]{:S(2)}, u32[]{:S(2)}) collective-permute-start(f32[3,128,128]{2,0,1:T(4,128)S(1)} %bitcast.94), channel_id=1, source_target_pairs={{0,1},{1,2},{2,3},{4,5},{5,6},{6,7},{8,9},{9,10},{10,11},{12,13},{... | collective-permute-start | bytes 589832 | tf_op jit(solution)/shard_map/ppermute | solution.py:10
where the time goes:
time: 187 us; the launch traced here: 186 us
  local copies, waits for them, and re-layouts  69.1 us (37%)
  blocking collectives  40.1 us (21%)
  matrix products  24.2 us (13%)
  starting transfers between devices  24.1 us (13%)
  other arithmetic  13.3 us (7%)
  waiting for transfers between devices  11.4 us (6%)
  between operations  4.13 us (2%)
    dynamic_update_slice x6, local copies, waits for them, and re-layouts, shards(): local_blocks = lax.map(sum_blocks, (elem_block, component_forces))  49.6 us
    psum x1, blocking collectives, shards(): energy = lax.psum(energy_part, ('dom', 'level')) / scale_total  40.1 us
    ppermute x10, starting transfers between devices, from_behind(): return lax.ppermute(block, axis, route)  24.1 us
    dot_general x3, matrix products, sum_blocks(): jnp.dot(selector, component_part, precision=lax.Precision.HIGHEST, prefer...  21.6 us
    ppermute x10, waiting for transfers between devices, from_behind(): return lax.ppermute(block, axis, route)  11.4 us
    scatter-add x1, other arithmetic, shards(): assembled = local_blocks.at[:, slot_blocks.reshape(-1), :].add(received)  8.79 us
    reshape x1, local copies, waits for them, and re-layouts, shards(): forces.reshape(elements, 3, block_size)  6.19 us
    unnamed x27, local copies, waits for them, and re-layouts  5.85 us
  transfers between devices with their start and end apart: 10, of which 3 were waited for; matrix products, arithmetic and copies ran while one was open for 49% of the time, Pallas kernels for 0%

commit v1 on v0

v1 whole, which is shorter than its diff:
```python
import functools

import jax
import jax.numpy as jnp
from jax import lax
from jax.experimental import pallas as pl
from jax.experimental.pallas import tpu as pltpu
from jax.sharding import PartitionSpec as P

MESH = pl.DeviceIdType.MESH
LANES = 128
CHUNKS = 4
M_ROWS = 512


def split_sum(pair):
    return pair[:, :LANES] + pair[:, LANES:]


def split(value):
    high = value.astype(jnp.bfloat16)
    low = (value - high.astype(jnp.float32)).astype(jnp.bfloat16)
    return jnp.concatenate([high, low], axis=1)


def mm(a, b):
    return jnp.dot(a, b, preferred_element_type=jnp.float32)


def column(row):
    n = row.shape[1]
    spot = lax.broadcasted_iota(jnp.int32, (n, n), 0) == lax.broadcasted_iota(jnp.int32, (n, n), 1)
    spread = jnp.where(spot, jnp.broadcast_to(row, (n, n)), 0.0)
    return jnp.sum(spread, axis=1, keepdims=True)


def body(
    R, L, scale,
    count_ref, mu_s, lam_s, cmu, clam, eb, share, hchild, hparent, dg_hbm,
    out_hbm, en_out,
    dg, F, coefs, eb16, outb, recv, chs, child, par_src, par, proj, en_l, en_r,
    dg_sem, out_sem, bx_s, bx_r, ch_s, ch_r, par_s, par_r, el_s, el_r, er_s, er_r,
):
    r = lax.axis_index("dom")
    l = lax.axis_index("level")
    E = dg.shape[0]
    comps, NB, _ = proj.shape
    S2, SL = share.shape
    half = S2 // 2
    H = hchild.shape[1]
    rows = E // CHUNKS
    slots = S2 * SL
    one = jnp.bfloat16(1.0)
    zero = jnp.bfloat16(0.0)

    def dom_peer(k):
        return lax.rem(r + k, R)

    def level_peer(k):
        return lax.rem(l + k, L)

    for i in range(CHUNKS):
        pltpu.make_async_copy(
            dg_hbm.at[pl.ds(i * rows, rows)], dg.at[pl.ds(i * rows, rows)], dg_sem.at[i]
        ).start()

    recv[...] = jnp.zeros_like(recv)
    child[...] = jnp.zeros_like(child)
    par[...] = jnp.full_like(par, -1)

    barrier = pltpu.get_barrier_semaphore()

    @pl.loop(1, R)
    def _(k):
        pl.semaphore_signal(barrier, inc=1, device_id=(dom_peer(k), l), device_id_type=MESH)

    @pl.loop(1, L)
    def _(k):
        pl.semaphore_signal(barrier, inc=1, device_id=(r, level_peer(k)), device_id_type=MESH)

    position = lax.broadcasted_iota(jnp.int32, cmu.shape, 0) * LANES + lax.broadcasted_iota(
        jnp.int32, cmu.shape, 1
    )
    live = position < count_ref[0]
    mu_rows = jnp.where(live, cmu[...], 0.0)
    lam_rows = jnp.where(live, clam[...], 0.0)
    for j in range(E // LANES):
        for which, table in enumerate((mu_rows, lam_rows)):
            coefs[which, j * LANES:(j + 1) * LANES, :] = jnp.broadcast_to(
                table[j:j + 1, :], (LANES, LANES)
            ).T
    for c in range(comps):
        eb16[c] = jnp.broadcast_to(eb[c:c + 1, :], (16, E)).astype(jnp.int16)
    par_src[...] = jnp.concatenate(
        [
            jnp.broadcast_to(hparent[:, 0:1], (H, LANES)),
            jnp.broadcast_to(hparent[:, 1:2], (H, LANES)),
        ],
        axis=0,
    )

    stiff = jnp.concatenate(
        [
            part[:, c * LANES:(c + 1) * LANES]
            for c in range(comps)
            for part in (mu_s[...], lam_s[...])
        ],
        axis=1,
    )
    energy = jnp.zeros((8, LANES), jnp.float32)
    for i in range(CHUNKS):
        span = slice(i * rows, (i + 1) * rows)
        pltpu.make_async_copy(
            dg_hbm.at[pl.ds(i * rows, rows)], dg.at[pl.ds(i * rows, rows)], dg_sem.at[i]
        ).wait()
        product = mm(dg[span, :], stiff)
        for c in range(comps):
            at = 2 * c * LANES
            force = (
                coefs[0, span, :] * product[:, at:at + LANES]
                + coefs[1, span, :] * product[:, at + LANES:at + 2 * LANES]
            )
            F[c, span, :] = split(force)
            work = force * dg[span, c * LANES:(c + 1) * LANES].astype(jnp.float32)
            energy = energy + jnp.sum(work.reshape(-1, 8, LANES), axis=0)

    pl.semaphore_wait(barrier, R + L - 2)

    def par_copy(target):
        return pltpu.make_async_remote_copy(
            src_ref=par_src, dst_ref=par, send_sem=par_s.at[0], recv_sem=par_r.at[0],
            device_id=(r, target), device_id_type=MESH,
        )

    @pl.when(l > 0)
    def _():
        par_copy(l - 1).start()

    en_l[l] = energy

    def en_l_copy(slot, peer, sem):
        return pltpu.make_async_remote_copy(
            src_ref=en_l.at[slot], dst_ref=en_l.at[slot], send_sem=el_s.at[sem],
            recv_sem=el_r.at[slot], device_id=(r, peer), device_id_type=MESH,
        )

    def en_r_copy(slot, peer, sem):
        return pltpu.make_async_remote_copy(
            src_ref=en_r.at[slot], dst_ref=en_r.at[slot], send_sem=er_s.at[sem],
            recv_sem=er_r.at[slot], device_id=(peer, l), device_id_type=MESH,
        )

    @pl.loop(1, L)
    def _(k):
        en_l_copy(l, level_peer(k), k).start()

    def selector(ids16, c):
        n = ids16.shape[0]
        pieces = []
        for k in range(E // LANES):
            key = jnp.tile(eb16[c, :, k * LANES:(k + 1) * LANES], (n // 16, 1))
            pieces.append(jnp.where(ids16 == key, one, zero))
        return jnp.concatenate(pieces, axis=1)

    def offset(o):
        return o + 1 if o < half else -(o - half + 1)

    def inside(o):
        partner = r + offset(o)
        return (partner >= 0) & (partner < R)

    def box_copy(c, o):
        opposite = (o + half) % S2
        return pltpu.make_async_remote_copy(
            src_ref=outb.at[c, pl.ds(o * SL, SL)],
            dst_ref=recv.at[c, pl.ds(opposite * SL, SL)],
            send_sem=bx_s.at[c, o], recv_sem=bx_r.at[c, opposite],
            device_id=(r + offset(o), l), device_id_type=MESH,
        )

    def box_wait(c, o):
        return pltpu.make_async_remote_copy(
            src_ref=outb.at[c, pl.ds(o * SL, SL)],
            dst_ref=recv.at[c, pl.ds(o * SL, SL)],
            send_sem=bx_s.at[c, o], recv_sem=bx_r.at[c, o],
            device_id=(r + offset(o), l), device_id_type=MESH,
        )

    share_f = share[...].astype(jnp.float32)
    share_col = jnp.concatenate([column(share_f[o:o + 1, :]) for o in range(S2)], axis=0)
    share16 = jnp.broadcast_to(share_col, (slots, LANES)).astype(jnp.int32).astype(jnp.int16)
    for c in range(comps):
        outb[c] = split_sum(mm(selector(share16, c), F[c]))
        for o in range(S2):
            @pl.when(inside(o))
            def _():
                box_copy(c, o).start()

    @pl.loop(1, L)
    def _(k):
        peer = level_peer(k)
        en_l_copy(peer, peer, k).wait_recv()

    en_r[r] = jnp.sum(en_l[...], axis=0)

    @pl.loop(1, R)
    def _(k):
        en_r_copy(r, dom_peer(k), k).start()

    @pl.when(l < L - 1)
    def _():
        par_copy(l).wait_recv()

    first16 = par[0:H, :].astype(jnp.int16)
    second16 = par[H:2 * H, :].astype(jnp.int16)
    own = []
    for c in range(comps):
        both = selector(first16, c) + selector(second16, c)
        own.append(split_sum(mm(both, F[c])))

    share_row = jnp.concatenate([share[o:o + 1, :] for o in range(S2)], axis=1)
    pair_hits = jnp.where(par[0:H, 0:1] == share_row, 1.0, 0.0) + jnp.where(
        par[H:2 * H, 0:1] == share_row, 1.0, 0.0
    )
    pair_hits = pair_hits.astype(jnp.bfloat16)

    row16 = lax.broadcasted_iota(jnp.int32, (M_ROWS, LANES), 0)

    def local(c):
        for m in range(NB // M_ROWS):
            ids16 = (row16 + m * M_ROWS).astype(jnp.int16)
            proj[c, m * M_ROWS:(m + 1) * M_ROWS, :] = split_sum(mm(selector(ids16, c), F[c]))

    def child_copy(c, target):
        return pltpu.make_async_remote_copy(
            src_ref=chs.at[c], dst_ref=child.at[c], send_sem=ch_s.at[c], recv_sem=ch_r.at[c],
            device_id=(r, target), device_id_type=MESH,
        )

    def pass_on(c):
        for o in range(S2):
            @pl.when(inside(o))
            def _():
                box_wait(c, o).wait_recv()
        chs[c] = 0.5 * (own[c] + split_sum(mm(pair_hits, split(recv[c]))))

        @pl.when(l < L - 1)
        def _():
            child_copy(c, l + 1).start()

    local(0)
    local(1)
    pass_on(0)
    pass_on(1)
    local(2)
    pass_on(2)

    row32 = lax.broadcasted_iota(jnp.int32, (NB, slots), 0)
    into = jnp.where(row32 == share_row, 1.0, 0.0).astype(jnp.bfloat16)
    hang = jnp.where(
        lax.broadcasted_iota(jnp.int32, (NB, H), 0) == hchild[...], 1.0, 0.0
    ).astype(jnp.bfloat16)
    keep = 1.0 - mm(hang, jnp.ones((H, LANES), jnp.bfloat16))
    for c in range(comps):
        full = (proj[c] + split_sum(mm(into, split(recv[c])))) * keep

        @pl.when(l > 0)
        def _():
            child_copy(c, l).wait_recv()

        proj[c] = full + split_sum(mm(hang, split(child[c])))
        pltpu.make_async_copy(proj.at[c], out_hbm.at[c], out_sem.at[c]).start()

    @pl.loop(1, R)
    def _(k):
        peer = dom_peer(k)
        en_r_copy(peer, peer, k).wait_recv()

    en_out[0, 0] = jnp.sum(en_r[...]) * 0.5 / jnp.float32(scale)

    @pl.loop(1, L)
    def _(k):
        en_l_copy(l, level_peer(k), k).wait_send()

    @pl.loop(1, R)
    def _(k):
        en_r_copy(r, dom_peer(k), k).wait_send()

    @pl.when(l > 0)
    def _():
        par_copy(l - 1).wait_send()

    for c in range(comps):
        for o in range(S2):
            @pl.when(inside(o))
            def _():
                box_copy(c, o).wait_send()

        @pl.when(l < L - 1)
        def _():
            child_copy(c, l + 1).wait_send()

        pltpu.make_async_copy(proj.at[c], out_hbm.at[c], out_sem.at[c]).wait()


def shards(
    R, L, dg_values, stiff_mu, stiff_lam, coef_mu, coef_lam, elem_count, elem_block,
    share_map, hang_child, hang_parent,
):
    E, D = dg_values.shape
    comps = elem_block.shape[0]
    NB = E // comps
    S2, SL = share_map.shape[1:]
    H = hang_child.shape[1]
    slots = S2 * SL
    f32, bf16, i32 = jnp.float32, jnp.bfloat16, jnp.int32
    dma = pltpu.SemaphoreType.DMA
    vmem = pl.BlockSpec(memory_space=pltpu.VMEM)
    smem = pl.BlockSpec(memory_space=pltpu.SMEM)
    hbm = pl.BlockSpec(memory_space=pl.ANY)
    projected, energy = pl.pallas_call(
        functools.partial(body, R, L, D * E * R * L),
        out_shape=(
            jax.ShapeDtypeStruct((comps, NB, LANES), f32),
            jax.ShapeDtypeStruct((1, 1), f32),
        ),
        in_specs=[smem] + [vmem] * 8 + [hbm],
        out_specs=(hbm, smem),
        scratch_shapes=[
            pltpu.VMEM((E, D), bf16),
            pltpu.VMEM((comps, E, 2 * LANES), bf16),
            pltpu.VMEM((2, E, LANES), f32),
            pltpu.VMEM((comps, 16, E), jnp.int16),
            pltpu.VMEM((comps, slots, LANES), f32),
            pltpu.VMEM((comps, slots, LANES), f32),
            pltpu.VMEM((comps, H, LANES), f32),
            pltpu.VMEM((comps, H, LANES), f32),
            pltpu.VMEM((2 * H, LANES), i32),
            pltpu.VMEM((2 * H, LANES), i32),
            pltpu.VMEM((comps, NB, LANES), f32),
            pltpu.VMEM((L, 8, LANES), f32),
            pltpu.VMEM((R, 8, LANES), f32),
            dma((CHUNKS,)), dma((comps,)),
            dma((comps, S2)), dma((comps, S2)),
            dma((comps,)), dma((comps,)),
            dma((1,)), dma((1,)),
            dma((L,)), dma((L,)),
            dma((R,)), dma((R,)),
        ],
        compiler_params=pltpu.CompilerParams(collective_id=0, has_side_effects=True),
        name="assembly",
    )(
        elem_count, stiff_mu, stiff_lam,
        coef_mu.reshape(-1, LANES), coef_lam.reshape(-1, LANES),
        elem_block, share_map[0], hang_child, hang_parent[0], dg_values,
    )
    return projected, energy.reshape(())


def solution(mesh):
    both = ("dom", "level")
    return jax.shard_map(
        functools.partial(shards, mesh.shape["dom"], mesh.shape["level"]),
        mesh=mesh,
        in_specs=(
            P(both, None), P(), P(), P(both), P(both), P(both), P(None, both),
            P(both, None, None), P(both, None), P(both, None, None),
        ),
        out_specs=(P(None, both, None), P()),
        check_vma=False,
    )
```

time: 187 us -> 31.3 us (0.17)
  the two profiles are of different devices: /device:TPU:18 before, /device:TPU:0 now
where the time goes in v1:
time: 31.3 us; the launch traced here: 31 us
  Pallas kernels  24 us (77%)
  local copies, waits for them, and re-layouts  4.03 us (13%)
  between operations  3.05 us (10%)
    pallas_call x1, Pallas kernels, shards(): pl.pallas_call(functools.partial(body, R, L, D * E * R * L), out_shape=(j...  24 us
    unnamed x1, local copies, waits for them, and re-layouts  2.65 us
    squeeze x1, local copies, waits for them, and re-layouts, shards(): hang_parent[0]  1.38 us

profile of v1, /device:TPU:0, one launch (start us, length us, event | category | flops | bytes accessed | tf_op | source)
XLA Modules:
  0.0 31.0 jit_solution(4693256066782557969)
XLA Ops:
  1.3 1.4 %copy.12.hparent = s32[64,2]{1,0:T(8,128)} copy(s32[64,2]{0,1:T(2,128)} %bitcast.8) | data formatting | bytes 1024 | tf_op jit(solution)/shard_map/squeeze | solution.py:355
  2.7 24.0 %assembly.1 = (f32[3,1024,128]{2,1,0:T(8,128)}, f32[1,1]{1,0:T(1,128)}) custom-call(s32[1]{0:T(128)S(6)} %copy.15.count_ref, bf16[384,384]{1,0:T(8,128)(2,1)} %mu_s.1, bf16[384,384]{1,0:T(8,128)(2,1)} %lam_s.1, f32[24,128]{1,0:T(8,128)} %bitcast.5, f32[24,128]{1,0:T(8,128)} %bitcast.6, s32[3,3072]{1,0:T(4,128)} %eb.1, s32[8,32]{1,0:T(8,128)} %bitcast.7, ...), custom_call_target="tpu_custom_call" | custom-call | tf_op jit(solution)/shard_map/assembly/pallas_call | solution.py:321
  26.6 2.7 %copy.16 = f32[3,1024,128]{2,1,0:T(8,128)} copy(f32[3,1024,128]{2,1,0:T(8,128)} %get-tuple-element.8) | data formatting | bytes 3145728

commit v2 on v1

v2 whole, which is shorter than its diff:
```python
import functools

import jax
import jax.numpy as jnp
from jax import lax
from jax.experimental import pallas as pl
from jax.experimental.pallas import tpu as pltpu
from jax.sharding import PartitionSpec as P

MESH = pl.DeviceIdType.MESH
LANES = 128
CHUNKS = 4
M_ROWS = 512
EARLY = 1


def split_sum(pair):
    return pair[:, :LANES] + pair[:, LANES:]


def split(value):
    high = value.astype(jnp.bfloat16)
    low = (value - high.astype(jnp.float32)).astype(jnp.bfloat16)
    return jnp.concatenate([high, low], axis=1)


def mm(a, b):
    return jnp.dot(a, b, preferred_element_type=jnp.float32)


def column(row):
    n = row.shape[1]
    spot = lax.broadcasted_iota(jnp.int32, (n, n), 0) == lax.broadcasted_iota(jnp.int32, (n, n), 1)
    spread = jnp.where(spot, jnp.broadcast_to(row, (n, n)), 0.0)
    return jnp.sum(spread, axis=1, keepdims=True)


def body(
    R, L, scale,
    count_hbm, mu_hbm, lam_hbm, cmu_hbm, clam_hbm, eb_hbm, share_hbm, hchild_hbm, hparent_hbm, dg_hbm,
    proj, en_out,
    count_ref, mu_s, lam_s, cmu, clam, eb, share, hchild, hparent, arg_sem,
    dg, F, own, energy_acc, eb16, outb, recv, chs, child, par_src, par, en_l, en_r,
    dg_sem, bx_s, bx_r, ch_s, ch_r, par_s, par_r, el_s, el_r, er_s, er_r,
):
    r = lax.axis_index("dom")
    l = lax.axis_index("level")
    E = dg.shape[0]
    comps, NB, _ = proj.shape
    S2, SL = share.shape
    half = S2 // 2
    H = hchild.shape[1]
    rows = E // CHUNKS
    slots = S2 * SL
    one = jnp.bfloat16(1.0)
    zero = jnp.bfloat16(0.0)

    def dom_peer(k):
        return lax.rem(r + k, R)

    def level_peer(k):
        return lax.rem(l + k, L)

    recv[...] = jnp.zeros_like(recv)
    child[...] = jnp.zeros_like(child)
    par[...] = jnp.full_like(par, -1)

    barrier = pltpu.get_barrier_semaphore()

    @pl.loop(1, R)
    def _(k):
        pl.semaphore_signal(barrier, inc=1, device_id=(dom_peer(k), l), device_id_type=MESH)

    @pl.loop(1, L)
    def _(k):
        pl.semaphore_signal(barrier, inc=1, device_id=(r, level_peer(k)), device_id_type=MESH)

    loads = [
        pltpu.make_async_copy(source, held, arg_sem.at[i])
        for i, (source, held) in enumerate([
            (mu_hbm, mu_s), (lam_hbm, lam_s), (cmu_hbm, cmu), (clam_hbm, clam),
            (count_hbm, count_ref), (eb_hbm, eb), (share_hbm, share),
            (hchild_hbm, hchild), (hparent_hbm, hparent),
        ])
    ]
    for load in loads:
        load.start()
    for i in range(CHUNKS):
        pltpu.make_async_copy(
            dg_hbm.at[pl.ds(i * rows, rows)], dg.at[pl.ds(i * rows, rows)], dg_sem.at[i]
        ).start()
    for load in loads:
        load.wait()

    for c in range(comps):
        eb16[c] = jnp.broadcast_to(eb[c:c + 1, :], (16, E)).astype(jnp.int16)
    par_src[...] = jnp.broadcast_to(
        jnp.concatenate(
            [column(hparent[which:which + 1, :].astype(jnp.float32)) for which in range(2)], axis=0
        ),
        (2 * H, LANES),
    ).astype(jnp.int32)

    stiff = jnp.concatenate(
        [
            part[:, c * LANES:(c + 1) * LANES]
            for c in range(comps)
            for part in (mu_s[...], lam_s[...])
        ],
        axis=1,
    )
    def spread(table, i):
        blocks = []
        for j in range(rows // LANES):
            at = i * (rows // LANES) + j
            live = lax.broadcasted_iota(jnp.int32, (1, LANES), 1) + at * LANES < count_ref[...]
            row = jnp.where(live, table[pl.ds(at, 1), :], 0.0)
            blocks.append(jnp.broadcast_to(row, (LANES, LANES)).T)
        return jnp.concatenate(blocks, axis=0)

    energy_acc[...] = jnp.zeros_like(energy_acc)

    @pl.loop(0, CHUNKS)
    def _(i):
        span = pl.ds(pl.multiple_of(i * rows, rows), rows)
        pltpu.make_async_copy(dg_hbm.at[span], dg.at[span], dg_sem.at[i]).wait()
        mu_wide, lam_wide = spread(cmu, i), spread(clam, i)
        part = dg[span, :]
        work = jnp.zeros((rows, LANES), jnp.float32)
        for c in range(comps):
            product = mm(part, stiff[:, 2 * c * LANES:2 * (c + 1) * LANES])
            force = mu_wide * product[:, :LANES] + lam_wide * product[:, LANES:]
            F[c, span, :] = split(force)
            work += force * part[:, c * LANES:(c + 1) * LANES].astype(jnp.float32)
        energy_acc[...] += jnp.sum(work.reshape(-1, 8, LANES), axis=0)

    def selector(ids16, c):
        n = ids16.shape[0]
        pieces = []
        for k in range(E // LANES):
            key = jnp.tile(eb16[c, :, k * LANES:(k + 1) * LANES], (n // 16, 1))
            pieces.append(jnp.where(ids16 == key, one, zero))
        return jnp.concatenate(pieces, axis=1)

    def offset(o):
        return o + 1 if o < half else -(o - half + 1)

    def inside(o):
        partner = r + offset(o)
        return (partner >= 0) & (partner < R)

    def box_copy(c, o):
        opposite = (o + half) % S2
        return pltpu.make_async_remote_copy(
            src_ref=outb.at[c, pl.ds(o * SL, SL)],
            dst_ref=recv.at[c, pl.ds(opposite * SL, SL)],
            send_sem=bx_s.at[c, o], recv_sem=bx_r.at[c, opposite],
            device_id=(r + offset(o), l), device_id_type=MESH,
        )

    def box_wait(c, o):
        return pltpu.make_async_remote_copy(
            src_ref=outb.at[c, pl.ds(o * SL, SL)],
            dst_ref=recv.at[c, pl.ds(o * SL, SL)],
            send_sem=bx_s.at[c, o], recv_sem=bx_r.at[c, o],
            device_id=(r + offset(o), l), device_id_type=MESH,
        )

    pl.semaphore_wait(barrier, R + L - 2)

    def par_copy(target):
        return pltpu.make_async_remote_copy(
            src_ref=par_src, dst_ref=par, send_sem=par_s.at[0], recv_sem=par_r.at[0],
            device_id=(r, target), device_id_type=MESH,
        )

    @pl.when(l > 0)
    def _():
        par_copy(l - 1).start()

    en_l[l] = energy_acc[...]

    def en_l_copy(slot, peer, sem):
        return pltpu.make_async_remote_copy(
            src_ref=en_l.at[slot], dst_ref=en_l.at[slot], send_sem=el_s.at[sem],
            recv_sem=el_r.at[slot], device_id=(r, peer), device_id_type=MESH,
        )

    def en_r_copy(slot, peer, sem):
        return pltpu.make_async_remote_copy(
            src_ref=en_r.at[slot], dst_ref=en_r.at[slot], send_sem=er_s.at[sem],
            recv_sem=er_r.at[slot], device_id=(peer, l), device_id_type=MESH,
        )

    @pl.loop(1, L)
    def _(k):
        en_l_copy(l, level_peer(k), k).start()

    share_f = share[...].astype(jnp.float32)
    share_col = jnp.concatenate([column(share_f[o:o + 1, :]) for o in range(S2)], axis=0)
    share16 = jnp.broadcast_to(share_col, (slots, LANES)).astype(jnp.int32).astype(jnp.int16)

    @pl.loop(0, comps)
    def _(c):
        outb[c] = split_sum(mm(selector(share16, c), F[c]))
        for o in range(S2):
            @pl.when(inside(o))
            def _():
                box_copy(c, o).start()

    per = NB // M_ROWS
    row16 = lax.broadcasted_iota(jnp.int32, (M_ROWS, LANES), 0)

    def local(step):
        c = step // per
        at = pl.multiple_of((step % per) * M_ROWS, M_ROWS)
        ids16 = (row16 + at).astype(jnp.int16)
        proj[c, pl.ds(at, M_ROWS), :] = split_sum(mm(selector(ids16, c), F[c]))

    def child_copy(c, target):
        return pltpu.make_async_remote_copy(
            src_ref=chs.at[c], dst_ref=child.at[c], send_sem=ch_s.at[c], recv_sem=ch_r.at[c],
            device_id=(r, target), device_id_type=MESH,
        )

    def pass_on(c):
        for o in range(S2):
            @pl.when(inside(o))
            def _():
                box_wait(c, o).wait_recv()
        chs[c] = 0.5 * (own[c] + split_sum(mm(pair_hits, split(recv[c]))))

        @pl.when(l < L - 1)
        def _():
            child_copy(c, l + 1).start()

    @pl.loop(0, per)
    def _(step):
        local(step)

    @pl.loop(1, L)
    def _(k):
        peer = level_peer(k)
        en_l_copy(peer, peer, k).wait_recv()

    en_r[r] = jnp.sum(en_l[...], axis=0)

    @pl.loop(1, R)
    def _(k):
        en_r_copy(r, dom_peer(k), k).start()

    @pl.loop(per, comps * per - EARLY)
    def _(step):
        local(step)

    @pl.when(l < L - 1)
    def _():
        par_copy(l).wait_recv()

    first16 = par[0:H, :].astype(jnp.int16)
    second16 = par[H:2 * H, :].astype(jnp.int16)
    @pl.loop(0, comps)
    def _(c):
        both = selector(first16, c) + selector(second16, c)
        own[c] = split_sum(mm(both, F[c]))


    share_row = jnp.concatenate([share[o:o + 1, :] for o in range(S2)], axis=1)
    pair_hits = jnp.where(par[0:H, 0:1] == share_row, 1.0, 0.0) + jnp.where(
        par[H:2 * H, 0:1] == share_row, 1.0, 0.0
    )
    pair_hits = pair_hits.astype(jnp.bfloat16)

    @pl.loop(0, comps)
    def _(c):
        pass_on(c)

    @pl.loop(comps * per - EARLY, comps * per)
    def _(step):
        local(step)

    row32 = lax.broadcasted_iota(jnp.int32, (NB, slots), 0)
    into = jnp.where(row32 == share_row, 1.0, 0.0).astype(jnp.bfloat16)
    hang = jnp.where(
        lax.broadcasted_iota(jnp.int32, (NB, H), 0) == hchild[...], 1.0, 0.0
    ).astype(jnp.bfloat16)
    keep = 1.0 - mm(hang, jnp.ones((H, LANES), jnp.bfloat16))
    @pl.loop(0, comps)
    def _(c):
        full = (proj[c] + split_sum(mm(into, split(recv[c])))) * keep

        @pl.when(l > 0)
        def _():
            child_copy(c, l).wait_recv()

        proj[c] = full + split_sum(mm(hang, split(child[c])))

    @pl.loop(1, R)
    def _(k):
        peer = dom_peer(k)
        en_r_copy(peer, peer, k).wait_recv()

    en_out[0, 0] = jnp.sum(en_r[...]) * 0.5 / jnp.float32(scale)

    @pl.loop(1, L)
    def _(k):
        en_l_copy(l, level_peer(k), k).wait_send()

    @pl.loop(1, R)
    def _(k):
        en_r_copy(r, dom_peer(k), k).wait_send()

    @pl.when(l > 0)
    def _():
        par_copy(l - 1).wait_send()

    @pl.loop(0, comps)
    def _(c):
        for o in range(S2):
            @pl.when(inside(o))
            def _():
                box_copy(c, o).wait_send()

        @pl.when(l < L - 1)
        def _():
            child_copy(c, l + 1).wait_send()


def shards(
    R, L, dg_values, stiff_mu, stiff_lam, coef_mu, coef_lam, elem_count, elem_block,
    share_map, hang_child, hang_parent,
):
    E, D = dg_values.shape
    comps = elem_block.shape[0]
    NB = E // comps
    S2, SL = share_map.shape[1:]
    H = hang_child.shape[1]
    slots = S2 * SL
    f32, bf16, i32 = jnp.float32, jnp.bfloat16, jnp.int32
    dma = pltpu.SemaphoreType.DMA
    vmem = pl.BlockSpec(memory_space=pltpu.VMEM)
    smem = pl.BlockSpec(memory_space=pltpu.SMEM)
    hbm = pl.BlockSpec(memory_space=pl.ANY)
    projected, energy = pl.pallas_call(
        functools.partial(body, R, L, D * E * R * L),
        out_shape=(
            pltpu.VMEM((comps, NB, LANES), f32),
            jax.ShapeDtypeStruct((1, 1), f32),
        ),
        in_specs=[hbm] * 10,
        out_specs=(vmem, smem),
        scratch_shapes=[
            pltpu.VMEM((1, 1), i32),
            pltpu.VMEM((D, D), bf16),
            pltpu.VMEM((D, D), bf16),
            pltpu.VMEM((E // LANES, LANES), f32),
            pltpu.VMEM((E // LANES, LANES), f32),
            pltpu.VMEM((comps, E), i32),
            pltpu.VMEM((S2, SL), i32),
            pltpu.VMEM((1, H), i32),
            pltpu.VMEM((2, H), i32),
            dma((9,)),
            pltpu.VMEM((E, D), bf16),
            pltpu.VMEM((comps, E, 2 * LANES), bf16),
            pltpu.VMEM((comps, H, LANES), f32),
            pltpu.VMEM((8, LANES), f32),
            pltpu.VMEM((comps, 16, E), jnp.int16),
            pltpu.VMEM((comps, slots, LANES), f32),
            pltpu.VMEM((comps, slots, LANES), f32),
            pltpu.VMEM((comps, H, LANES), f32),
            pltpu.VMEM((comps, H, LANES), f32),
            pltpu.VMEM((2 * H, LANES), i32),
            pltpu.VMEM((2 * H, LANES), i32),
            pltpu.VMEM((L, 8, LANES), f32),
            pltpu.VMEM((R, 8, LANES), f32),
            dma((CHUNKS,)),
            dma((comps, S2)), dma((comps, S2)),
            dma((comps,)), dma((comps,)),
            dma((1,)), dma((1,)),
            dma((L,)), dma((L,)),
            dma((R,)), dma((R,)),
        ],
        compiler_params=pltpu.CompilerParams(collective_id=0, has_side_effects=True),
        name="assembly",
    )(
        elem_count.reshape(1, 1), stiff_mu, stiff_lam,
        coef_mu.reshape(-1, LANES), coef_lam.reshape(-1, LANES),
        elem_block, share_map[0], hang_child, hang_parent[0].T, dg_values,
    )
    return projected, energy.reshape(())


def solution(mesh):
    both = ("dom", "level")
    return jax.shard_map(
        functools.partial(shards, mesh.shape["dom"], mesh.shape["level"]),
        mesh=mesh,
        in_specs=(
            P(both, None), P(), P(), P(both), P(both), P(both), P(None, both),
            P(both, None, None), P(both, None), P(both, None, None),
        ),
        out_specs=(P(None, both, None), P()),
        check_vma=False,
    )
```

time: 31.3 us -> 27.4 us (0.88)
  local copies, waits for them, and re-layouts: 4.03 us -> 1.15 us
  Pallas kernels: 24 us -> 23.1 us
    unnamed x1, local copies, waits for them, and re-layouts: 2.65 us -> 1.15 us
    squeeze x1 -> x0, local copies, waits for them, and re-layouts: 1.38 us -> none  [shards(): hang_parent[0]]
    pallas_call x1, Pallas kernels: 24 us -> 23.1 us  [shards(): pl.pallas_call(functools.partial(body, R, L, D * E * R * L), out_shape=(p...]
where the time goes in v2:
time: 27.4 us; the launch traced here: 27.3 us
  Pallas kernels  23.1 us (84%)
  between operations  2.98 us (11%)
  local copies, waits for them, and re-layouts  1.15 us (4%)
    pallas_call x1, Pallas kernels, shards(): pl.pallas_call(functools.partial(body, R, L, D * E * R * L), out_shape=(p...  23.1 us
    unnamed x1, local copies, waits for them, and re-layouts  1.15 us

profile of v2, /device:TPU:0, one launch (start us, length us, event | category | flops | bytes accessed | tf_op | source)
XLA Modules:
  0.0 27.3 jit_solution(15468838886850908773)
XLA Ops:
  1.3 23.1 %assembly.1 = (f32[3,1024,128]{2,1,0:T(8,128)S(1)}, f32[1,1]{1,0:T(1,128)}) custom-call(s32[1,1]{1,0:T(1,128)} %bitcast.8.count_hbm, bf16[384,384]{1,0:T(8,128)(2,1)} %mu_hbm.1, bf16[384,384]{1,0:T(8,128)(2,1)} %lam_hbm.1, f32[24,128]{1,0:T(8,128)} %bitcast.9, f32[24,128]{1,0:T(8,128)} %bitcast.10, s32[3,3072]{1,0:T(4,128)} %eb_hbm.1, s32[8,32]{1,0:T(8,128)} %bitcast.11, ...), custom_call_target="tpu_custom_call" | custom-call | tf_op jit(solution)/shard_map/assembly/pallas_call | solution.py:344
  24.4 1.1 %copy.14 = f32[3,1024,128]{2,1,0:T(8,128)} copy(f32[3,1024,128]{2,1,0:T(8,128)S(1)} %get-tuple-element.6) | data formatting | bytes 3145728
